TPU v7x, 32 devices: a whole 2x2x4 slice. The times are simulated.
32 devices in a mesh: zero: 4 (over z), model: 4 (over x, core), trial: 2 (over y).
Axes of the slice: x: 2, y: 2, z: 4, core: 2. Of those that a mesh axis runs over, the one named last changes fastest.
Arguments:
- w_query: bfloat16 [4096, 2048], P(('trial', 'zero'), 'model'), parts along dimension 0, may hold values from -0.125 to 0.125
- low_query: bfloat16 [4096, 32], P(('trial', 'zero')), parts along dimension 0, may hold values from -0.125 to 0.125
- high_query: bfloat16 [64, 2048], P('trial', 'model'), parts along dimension 0, may hold values from -1 to 1
- w_key: bfloat16 [4096, 512], P(('trial', 'zero'), 'model'), parts along dimension 0, may hold values from -0.125 to 0.125
- low_key: bfloat16 [4096, 32], P(('trial', 'zero')), parts along dimension 0, may hold values from -0.125 to 0.125
- high_key: bfloat16 [64, 512], P('trial', 'model'), parts along dimension 0, may hold values from -1 to 1
- w_value: bfloat16 [4096, 512], P(('trial', 'zero'), 'model'), parts along dimension 0, may hold values from -0.125 to 0.125
- low_value: bfloat16 [4096, 32], P(('trial', 'zero')), parts along dimension 0, may hold values from -0.125 to 0.125
- high_value: bfloat16 [64, 512], P('trial', 'model'), parts along dimension 0, may hold values from -1 to 1
- w_mixed: bfloat16 [4096, 2048], P(('trial', 'model'), 'zero'), parts along dimension 0, may hold values from -0.125 to 0.125
- low_mixed: bfloat16 [4096, 32], P(('trial', 'model')), parts along dimension 0, may hold values from -0.125 to 0.125
- high_mixed: bfloat16 [64, 2048], P('trial', 'zero'), parts along dimension 0, may hold values from -1 to 1
- norm_train: float32 [4096], P(('trial', 'zero', 'model')), parts along dimension 0, may hold values from 0.25 to 1.75
- norm_step: float32 [4096], P(('trial', 'zero', 'model')), parts along dimension 0, may hold values from -0.3 to 0.3
Outputs:
- final_query: bfloat16 [4096, 2048], P('trial', 'model'), parts along dimension 0
- final_key: bfloat16 [4096, 512], P('trial', 'model'), parts along dimension 0
- final_value: bfloat16 [4096, 512], P('trial', 'model'), parts along dimension 0
- final_mixed: bfloat16 [4096, 2048], P(('trial', 'model')), parts along dimension 0
- serve_norm: bfloat16 [4096], P('trial'), parts along dimension 0
There are 2 independent parts, one for each index of `trial`. A program takes and returns all parts, laid end to end along the dimension named above; each array names one. Nothing has to cross between parts.
All inputs are finite; a program needn't handle non-finite values.
Results may differ from a plain program's by a relative error of at most 0.001.
Values may be sent and summed in bfloat16 or wider, within the bound.
A program may use at most 64 MiB of HBM per device.

v0:
```python
import jax
import jax.numpy as jnp
from jax import lax
from jax.sharding import PartitionSpec as P

mix_rate = 2.0


def shards(
    w_query,
    low_query,
    high_query,
    w_key,
    low_key,
    high_key,
    w_value,
    low_value,
    high_value,
    w_mixed,
    low_mixed,
    high_mixed,
    norm_train,
    norm_step,
):
    result_query = w_query.astype(jnp.float32) + mix_rate * jnp.dot(
        low_query, high_query, preferred_element_type=jnp.float32
    )
    result_key = w_key.astype(jnp.float32) + mix_rate * jnp.dot(
        low_key, high_key, preferred_element_type=jnp.float32
    )
    result_value = w_value.astype(jnp.float32) + mix_rate * jnp.dot(
        low_value, high_value, preferred_element_type=jnp.float32
    )
    result_mixed = w_mixed.astype(jnp.float32) + mix_rate * jnp.dot(
        low_mixed, high_mixed, preferred_element_type=jnp.float32
    )
    narrow_query, narrow_key, narrow_value, narrow_mixed = (
        result_query.astype(jnp.bfloat16),
        result_key.astype(jnp.bfloat16),
        result_value.astype(jnp.bfloat16),
        result_mixed.astype(jnp.bfloat16),
    )
    final_query, final_key, final_value, final_mixed = (
        lax.all_gather(narrow_query, "zero", axis=0, tiled=True),
        lax.all_gather(narrow_key, "zero", axis=0, tiled=True),
        lax.all_gather(narrow_value, "zero", axis=0, tiled=True),
        lax.all_gather(narrow_mixed, "zero", axis=1, tiled=True),
    )
    serve_norm = lax.all_gather(
        (norm_train + norm_step).astype(jnp.bfloat16), ("zero", "model"), axis=0, tiled=True
    )
    return (final_query, final_key, final_value, final_mixed, serve_norm)


def solution(mesh):
    placed = (
        P(("trial", "zero"), "model"),
        P(("trial", "zero"), None),
        P("trial", "model"),
        P(("trial", "zero"), "model"),
        P(("trial", "zero"), None),
        P("trial", "model"),
        P(("trial", "zero"), "model"),
        P(("trial", "zero"), None),
        P("trial", "model"),
        P(("trial", "model"), "zero"),
        P(("trial", "model"), None),
        P("trial", "zero"),
        P(("trial", "zero", "model")),
        P(("trial", "zero", "model")),
    )
    return jax.shard_map(
        shards,
        mesh=mesh,
        in_specs=placed,
        out_specs=(
            P("trial", "model"),
            P("trial", "model"),
            P("trial", "model"),
            P(("trial", "model"), None),
            P("trial"),
        ),
        check_vma=False,
    )
```

profile of v0, /device:TPU:0, one launch (start us, length us, event | category | flops | bytes accessed | tf_op | source)
XLA Modules:
  0.0 131.7 jit_solution(212639038545267897)
XLA Ops:
  7.2 0.0 copy-start
  7.2 0.0 copy-start.2
  7.2 0.0 copy-start.4
  7.2 0.0 copy-start.6
  7.2 0.0 copy-start.3
  7.2 0.0 copy-start.5
  7.2 0.0 copy-start.7
  7.2 0.0 all-gather.4.cloned.1.call-start
  7.3 0.6 copy-done
  7.9 2.2 %fusion.2 = bf16[512,512]{1,0:T(8,128)(2,1)} fusion(bf16[512,32]{0,1:T(8,128)(2,1)S(1)} %copy-done, bf16[32,512]{1,0:T(8,128)(2,1)} %param.16, bf16[512,512]{1,0:T(8,128)(2,1)} %param.14), kind=kOutput, calls=%fused_computation.4 | convolution fusion | flops 17825792 | bytes 1114112 | tf_op jit(solution)/shard_map/dot_general | solution.py:25
  10.1 0.0 all-gather.4.cloned.1.call-update
  10.1 0.0 all-gather.6.cloned.1.call-start
  10.2 2.2 %fusion.3 = bf16[512,512]{1,0:T(8,128)(2,1)} fusion(bf16[512,32]{0,1:T(8,128)(2,1)} %param.24, bf16[32,512]{1,0:T(8,128)(2,1)} %param.25, bf16[512,512]{1,0:T(8,128)(2,1)} %param.23), kind=kOutput, calls=%fused_computation.5 | convolution fusion | flops 17825792 | bytes 1114112 | tf_op jit(solution)/shard_map/dot_general | solution.py:34
  12.4 0.0 all-gather.6.cloned.1.call-update
  12.4 0.0 copy-done.2
  12.4 0.0 copy-done.4
  12.4 0.0 copy-done.6
  12.4 0.2 fusion.6
  12.7 23.1 %all_gather.16 = bf16[2048,128]{1,0:T(8,128)(2,1)S(1)} all-gather(bf16[512,128]{1,0:T(8,128)(2,1)S(1)} %fusion.6), channel_id=1, replica_groups=mesh['zero'=4,'model'=4,'trial'=2] {'zero'}, dimensions={0}, use_global_device_ids=true | all-gather | bytes 655360 | tf_op jit(solution)/shard_map/all_gather | solution.py:45
  35.8 0.0 copy-done.3
  35.8 0.0 copy-done.5
  35.8 0.2 fusion.7
  36.0 21.4 %all_gather.17 = bf16[2048,128]{1,0:T(8,128)(2,1)S(1)} all-gather(bf16[512,128]{1,0:T(8,128)(2,1)S(1)} %fusion.7), channel_id=1, replica_groups=mesh['zero'=4,'model'=4,'trial'=2] {'zero'}, dimensions={0}, use_global_device_ids=true | all-gather | bytes 655360 | tf_op jit(solution)/shard_map/all_gather | solution.py:46
  57.4 0.0 copy-done.9
  57.4 20.5 %all-gather = bf16[16,1,128]{2,1,0:T(2,128)(2,1)S(1)} all-gather(bf16[1,1,128]{2,1,0:T(2,128)(2,1)S(1)} %convert_bitcast_fusion), channel_id=1, replica_groups=mesh['zero'=4,'model'=4,'trial'=2] {'zero','model'}, dimensions={0}, use_global_device_ids=true | all-gather | bytes 4352 | tf_op jit(solution)/shard_map/all_gather | solution.py:49
  77.9 0.6 reduce
  78.5 40.3 %all-gather.6.cloned.1.call-done = bf16[512,2048]{1,0:T(8,128)(2,1)} async-done(((bf16[512,512]{1,0:T(8,128)(2,1)}), bf16[512,2048]{1,0:T(8,128)(2,1)}) %all-gather.6.cloned.1.call-update) | async-done | bytes 2097168 | tf_op jit(solution)/shard_map/all_gather | solution.py:47
  118.8 3.2 %copy.23 = bf16[2048,512]{1,0:T(8,128)(2,1)} copy(bf16[2048,512]{1,0:T(8,128)(2,1)} %all-gather.4.cloned.1.call-done) | data formatting | bytes 4194304
  122.0 0.8 copy.24
  122.8 0.8 copy.25
  123.6 0.0 copy-done.1
  123.6 1.3 %copy.26 = bf16[512,2048]{1,0:T(8,128)(2,1)} copy(bf16[512,2048]{1,0:T(8,128)(2,1)S(1)} %copy-done.1) | data formatting | bytes 4194304
  (7 shorter events, 0.0 us)
Async XLA Ops:
  7.2 0.8 copy-start
  7.2 5.2 %copy-start.2 = (bf16[512,128]{1,0:T(8,128)(2,1)S(1)}, bf16[512,128]{1,0:T(8,128)(2,1)}, u32[]{:S(2)}) copy-start(bf16[512,128]{1,0:T(8,128)(2,1)} %param.17) | copy-start | bytes 393220
  7.2 5.2 %copy-start.4 = (bf16[512,32]{0,1:T(8,128)(2,1)S(1)}, bf16[512,32]{0,1:T(8,128)(2,1)}, u32[]{:S(2)}) copy-start(bf16[512,32]{0,1:T(8,128)(2,1)} %param.18) | copy-start | bytes 98308
  7.2 5.2 %copy-start.6 = (bf16[32,128]{1,0:T(8,128)(2,1)S(1)}, bf16[32,128]{1,0:T(8,128)(2,1)}, u32[]{:S(2)}) copy-start(bf16[32,128]{1,0:T(8,128)(2,1)} %param.19) | copy-start | bytes 24580
  7.2 28.6 %copy-start.3 = (bf16[512,128]{1,0:T(8,128)(2,1)S(1)}, bf16[512,128]{1,0:T(8,128)(2,1)}, u32[]{:S(2)}) copy-start(bf16[512,128]{1,0:T(8,128)(2,1)} %param.20) | copy-start | bytes 393220
  7.2 28.6 %copy-start.5 = (bf16[512,32]{0,1:T(8,128)(2,1)S(1)}, bf16[512,32]{0,1:T(8,128)(2,1)}, u32[]{:S(2)}) copy-start(bf16[512,32]{0,1:T(8,128)(2,1)} %param.21) | copy-start | bytes 98308
  7.2 28.5 %copy-start.7 = (bf16[32,128]{1,0:T(8,128)(2,1)S(1)}, bf16[32,128]{1,0:T(8,128)(2,1)}, u32[]{:S(2)}) copy-start(bf16[32,128]{1,0:T(8,128)(2,1)} %param.22) | copy-start | bytes 24580
  7.2 71.2 %all-gather.4.cloned.1.call-start = ((), (), s32[]{:S(2)}) async-start(), calls=%async_computation | async-start | bytes 2621440 | tf_op jit(solution)/shard_map/all_gather | solution.py:44
  10.1 47.3 %copy-start.8 = (f32[128]{0:T(128)S(1)}, f32[128]{0:T(128)}, u32[]{:S(2)}) copy-start(f32[128]{0:T(128)} %param.26) | copy-start | bytes 1540
  10.1 47.3 %copy-start.9 = (f32[128]{0:T(128)S(1)}, f32[128]{0:T(128)}, u32[]{:S(2)}) copy-start(f32[128]{0:T(128)} %param.27) | copy-start | bytes 1540
  10.1 108.7 %all-gather.6.cloned.1.call-start = ((), (), s32[]{:S(2)}) async-start(), calls=%async_computation.1 | async-start | bytes 2621440 | tf_op jit(solution)/shard_map/all_gather | solution.py:47
  118.8 4.8 %copy-start.1 = (bf16[512,2048]{1,0:T(8,128)(2,1)S(1)}, bf16[512,2048]{1,0:T(8,128)(2,1)}, u32[]{:S(2)}) copy-start(bf16[512,2048]{1,0:T(8,128)(2,1)} %all-gather.6.cloned.1.call-done) | copy-start | bytes 6291460
Sparse Core Ops, SparseCore 0:
  10.3 60.5 all-gather.3
  73.0 45.7 all-gather.5
where the time goes:
time: 132 us
  blocking collectives  65 us (49%)
  waiting for transfers between devices  40.3 us (31%)
  between operations  14.2 us (11%)
  local copies, waits for them, and re-layouts  6.78 us (5%)
  matrix products  4.8 us (4%)
    all_gather x1, waiting for transfers between devices, shards(): lax.all_gather(narrow_mixed, 'zero', axis=1, tiled=True)  40.3 us
    all_gather x1, blocking collectives, shards(): lax.all_gather(narrow_key, 'zero', axis=0, tiled=True)  23.1 us
    all_gather x1, blocking collectives, shards(): lax.all_gather(narrow_value, 'zero', axis=0, tiled=True)  21.4 us
    all_gather x1, blocking collectives, shards(): lax.all_gather((norm_train + norm_step).astype(jnp.bfloat16), ('zero', 'm...  20.5 us
    unnamed x24, local copies, waits for them, and re-layouts  6.78 us
  transfers between devices with their start and end apart: 2, of which 1 were waited for; matrix products, arithmetic and copies ran while one was open for 2% of the time, Pallas kernels for 0%

commit v1 on v0

--- a/solution.py
+++ b/solution.py
@@ -4,6 +4,11 @@
 from jax.sharding import PartitionSpec as P
 
 mix_rate = 2.0
+
+
+def gathered_along(value, axis, dim):
+    shards = lax.all_gather(value, axis)
+    return jnp.concatenate(shards, axis=dim)
 
 
 def shards(
@@ -44,7 +49,7 @@
         lax.all_gather(narrow_query, "zero", axis=0, tiled=True),
         lax.all_gather(narrow_key, "zero", axis=0, tiled=True),
         lax.all_gather(narrow_value, "zero", axis=0, tiled=True),
-        lax.all_gather(narrow_mixed, "zero", axis=1, tiled=True),
+        gathered_along(narrow_mixed, "zero", 1),
     )
     serve_norm = lax.all_gather(
         (norm_train + norm_step).astype(jnp.bfloat16), ("zero", "model"), axis=0, tiled=True

time: 132 us -> 131 us (level)
  waiting for transfers between devices: 40.3 us -> 37 us
  local copies, waits for them, and re-layouts: 6.78 us -> 8.64 us
    all_gather x1, waiting for transfers between devices: 40.3 us -> 0.01 us  [gathered_along(): shards = lax.all_gather(value, axis)]
    all_gather x1, waiting for transfers between devices: 0.01 us -> 37 us  [shards(): lax.all_gather(narrow_query, 'zero', axis=0, tiled=True)]
    reshape x0 -> x1, local copies, waits for them, and re-layouts: none -> 3.33 us  [gathered_along(): return jnp.concatenate(shards, axis=dim)]
    unnamed x24 -> x21, local copies, waits for them, and re-layouts: 6.78 us -> 5.31 us
  transfers between devices with their start and end apart: 2 -> 2, of which waited for: 1 -> 1; matrix products, arithmetic and copies ran while one was open for 2% -> 5% of each run, Pallas kernels for 0% -> 0%
where the time goes in v1:
time: 131 us; the launch traced here: 130 us
  blocking collectives  65 us (50%)
  waiting for transfers between devices  37 us (28%)
  between operations  14.2 us (11%)
  local copies, waits for them, and re-layouts  8.64 us (7%)
  matrix products  4.8 us (4%)
    all_gather x1, waiting for transfers between devices, shards(): lax.all_gather(narrow_query, 'zero', axis=0, tiled=True)  37 us
    all_gather x1, blocking collectives, shards(): lax.all_gather(narrow_key, 'zero', axis=0, tiled=True)  23.1 us
    all_gather x1, blocking collectives, shards(): lax.all_gather(narrow_value, 'zero', axis=0, tiled=True)  21.4 us
    all_gather x1, blocking collectives, shards(): lax.all_gather((norm_train + norm_step).astype(jnp.bfloat16), ('zero', 'm...  20.5 us
    unnamed x21, local copies, waits for them, and re-layouts  5.31 us
    reshape x1, local copies, waits for them, and re-layouts, gathered_along(): return jnp.concatenate(shards, axis=dim)  3.33 us
  transfers between devices with their start and end apart: 2, of which 1 were waited for; matrix products, arithmetic and copies ran while one was open for 5% of the time, Pallas kernels for 0%

profile of v1, /device:TPU:0, one launch (start us, length us, event | category | flops | bytes accessed | tf_op | source)
XLA Modules:
  0.0 130.3 jit_solution(15425311209474036477)
XLA Ops:
  7.2 0.0 copy-start
  7.2 0.0 copy-start.1
  7.2 0.0 copy-start.3
  7.2 0.0 copy-start.5
  7.2 0.0 copy-start.2
  7.2 0.0 copy-start.4
  7.2 0.0 copy-start.6
  7.2 0.0 all-gather.7.cloned.1.call-start
  7.3 0.6 copy-done
  7.9 2.2 %fusion.3 = bf16[512,512]{1,0:T(8,128)(2,1)} fusion(bf16[512,32]{0,1:T(8,128)(2,1)S(1)} %copy-done, bf16[32,512]{1,0:T(8,128)(2,1)} %param.25, bf16[512,512]{1,0:T(8,128)(2,1)} %param.23), kind=kOutput, calls=%fused_computation.5 | convolution fusion | flops 17825792 | bytes 1114112 | tf_op jit(solution)/shard_map/dot_general | solution.py:39
  10.1 0.0 all-gather.7.cloned.1.call-update
  10.1 0.0 all-gather.5.cloned.1.call-start
  10.2 2.2 %fusion.2 = bf16[512,512]{1,0:T(8,128)(2,1)} fusion(bf16[512,32]{0,1:T(8,128)(2,1)} %param.15, bf16[32,512]{1,0:T(8,128)(2,1)} %param.16, bf16[512,512]{1,0:T(8,128)(2,1)} %param.14), kind=kOutput, calls=%fused_computation.4 | convolution fusion | flops 17825792 | bytes 1114112 | tf_op jit(solution)/shard_map/dot_general | solution.py:30
  12.4 0.0 all-gather.5.cloned.1.call-update
  12.4 0.0 copy-done.1
  12.4 0.0 copy-done.3
  12.4 0.0 copy-done.5
  12.4 0.2 fusion.6
  12.7 23.1 %all_gather.19 = bf16[2048,128]{1,0:T(8,128)(2,1)S(1)} all-gather(bf16[512,128]{1,0:T(8,128)(2,1)S(1)} %fusion.6), channel_id=1, replica_groups=mesh['zero'=4,'model'=4,'trial'=2] {'zero'}, dimensions={0}, use_global_device_ids=true | all-gather | bytes 655360 | tf_op jit(solution)/shard_map/all_gather | solution.py:50
  35.8 0.0 copy-done.2
  35.8 0.0 copy-done.4
  35.8 0.0 copy-done.6
  35.8 0.2 fusion.7
  36.0 21.4 %all_gather.20 = bf16[2048,128]{1,0:T(8,128)(2,1)S(1)} all-gather(bf16[512,128]{1,0:T(8,128)(2,1)S(1)} %fusion.7), channel_id=1, replica_groups=mesh['zero'=4,'model'=4,'trial'=2] {'zero'}, dimensions={0}, use_global_device_ids=true | all-gather | bytes 655360 | tf_op jit(solution)/shard_map/all_gather | solution.py:51
  57.4 0.0 copy-done.7
  57.4 20.5 %all-gather.1 = bf16[16,1,128]{2,1,0:T(2,128)(2,1)S(1)} all-gather(bf16[1,1,128]{2,1,0:T(2,128)(2,1)S(1)} %convert_bitcast_fusion), channel_id=1, replica_groups=mesh['zero'=4,'model'=4,'trial'=2] {'zero','model'}, dimensions={0}, use_global_device_ids=true | all-gather | bytes 4352 | tf_op jit(solution)/shard_map/all_gather | solution.py:54
  77.9 0.6 reduce
  78.5 3.3 %copy.22 = bf16[4,64,8,512]{3,2,0,1:T(8,128)(2,1)} copy(bf16[4,64,8,512]{3,2,1,0:T(8,128)(2,1)} %bitcast.16) | data formatting | bytes 4194304 | tf_op jit(solution)/shard_map/reshape | solution.py:11
  81.8 37.0 %all-gather.5.cloned.1.call-done = bf16[2048,512]{1,0:T(8,128)(2,1)} async-done(((bf16[512,512]{1,0:T(8,128)(2,1)}), bf16[2048,512]{1,0:T(8,128)(2,1)}) %all-gather.5.cloned.1.call-update) | async-done | bytes 2097168 | tf_op jit(solution)/shard_map/all_gather | solution.py:49
  118.8 3.0 %copy.26 = bf16[2048,512]{1,0:T(8,128)(2,1)} copy(bf16[2048,512]{1,0:T(8,128)(2,1)} %all-gather.5.cloned.1.call-done) | data formatting | bytes 4194304
  121.9 0.8 copy.27
  122.6 0.8 copy.28
  (5 shorter events, 0.0 us)
Async XLA Ops:
  7.2 0.8 copy-start
  7.2 5.2 %copy-start.1 = (bf16[512,128]{1,0:T(8,128)(2,1)S(1)}, bf16[512,128]{1,0:T(8,128)(2,1)}, u32[]{:S(2)}) copy-start(bf16[512,128]{1,0:T(8,128)(2,1)} %param.17) | copy-start | bytes 393220
  7.2 5.2 %copy-start.3 = (bf16[512,32]{0,1:T(8,128)(2,1)S(1)}, bf16[512,32]{0,1:T(8,128)(2,1)}, u32[]{:S(2)}) copy-start(bf16[512,32]{0,1:T(8,128)(2,1)} %param.18) | copy-start | bytes 98308
  7.2 5.2 %copy-start.5 = (bf16[32,128]{1,0:T(8,128)(2,1)S(1)}, bf16[32,128]{1,0:T(8,128)(2,1)}, u32[]{:S(2)}) copy-start(bf16[32,128]{1,0:T(8,128)(2,1)} %param.19) | copy-start | bytes 24580
  7.2 28.6 %copy-start.2 = (bf16[512,128]{1,0:T(8,128)(2,1)S(1)}, bf16[512,128]{1,0:T(8,128)(2,1)}, u32[]{:S(2)}) copy-start(bf16[512,128]{1,0:T(8,128)(2,1)} %param.20) | copy-start | bytes 393220
  7.2 28.6 %copy-start.4 = (bf16[512,32]{0,1:T(8,128)(2,1)S(1)}, bf16[512,32]{0,1:T(8,128)(2,1)}, u32[]{:S(2)}) copy-start(bf16[512,32]{0,1:T(8,128)(2,1)} %param.21) | copy-start | bytes 98308
  7.2 28.5 %copy-start.6 = (bf16[32,128]{1,0:T(8,128)(2,1)S(1)}, bf16[32,128]{1,0:T(8,128)(2,1)}, u32[]{:S(2)}) copy-start(bf16[32,128]{1,0:T(8,128)(2,1)} %param.22) | copy-start | bytes 24580
  7.2 71.3 %all-gather.7.cloned.1.call-start = ((), (), s32[]{:S(2)}) async-start(), calls=%async_computation.1 | async-start | bytes 2621440 | tf_op jit(solution)/shard_map/all_gather | solution.py:10
  10.1 47.3 %copy-start.7 = (f32[128]{0:T(128)S(1)}, f32[128]{0:T(128)}, u32[]{:S(2)}) copy-start(f32[128]{0:T(128)} %param.26) | copy-start | bytes 1540
  10.1 47.3 %copy-start.8 = (f32[128]{0:T(128)S(1)}, f32[128]{0:T(128)}, u32[]{:S(2)}) copy-start(f32[128]{0:T(128)} %param.27) | copy-start | bytes 1540
  10.1 108.7 %all-gather.5.cloned.1.call-start = ((), (), s32[]{:S(2)}) async-start(), calls=%async_computation | async-start | bytes 2621440 | tf_op jit(solution)/shard_map/all_gather | solution.py:49
Sparse Core Ops, SparseCore 0:
  10.3 60.5 all-gather.6
  73.0 45.7 all-gather.4
